TPU v7x, 32 devices: a 4x4x1 block of a 4x4x8 slice. The times are simulated.
32 devices in a mesh: dp: 2 (over z, core), ep: 16 (over x, y).
Axes of the slice: x: 4, y: 4, z: 1, core: 2. Of those that a mesh axis runs over, the one named last changes fastest.
The devices are a block of a 4x4x8 slice.
Arguments:
- x: bfloat16 [2, 16, 256, 3072], P('dp', 'ep'), parts along dimension 0
- expert: int32 [2, 16, 256, 4], P('dp', 'ep'), parts along dimension 0
- slot: int32 [2, 16, 256, 4], P('dp', 'ep'), parts along dimension 0
- gate: float32 [2, 16, 256, 4], P('dp', 'ep'), parts along dimension 0
- w_gate: bfloat16 [16, 3072, 10752], P('ep')
- w_up: bfloat16 [16, 3072, 10752], P('ep')
- w_down: bfloat16 [16, 10752, 3072], P('ep')
Outputs:
- y: bfloat16 [2, 16, 256, 3072], P('dp', 'ep'), parts along dimension 0
There are 2 independent parts. A program takes and returns all parts, laid end to end along the dimension named above; an argument that names none is the same for every part.
All inputs are finite; a program needn't handle non-finite values.
Results may differ from a plain program's by a relative error of at most 0.009.
Values are sent between devices in bfloat16 or wider.
A program may use at most 768 MiB of HBM per device.

v0:
```python
import jax
import jax.numpy as jnp
from jax import lax
from jax.sharding import NamedSharding, PartitionSpec as P


def einsum(form, a, b):
    return jnp.einsum(form, a.astype(jnp.float32), b.astype(jnp.float32))


def solution(mesh):
    def placed(v, *spec):
        return lax.with_sharding_constraint(v, NamedSharding(mesh, P(*spec)))

    def step(x, expert, slot, gate, w_gate, w_up, w_down):
        experts, (tokens, top) = w_gate.shape[0], expert.shape[2:]
        slots = 5 * tokens * top // (4 * experts)
        to_expert = jax.nn.one_hot(expert, experts, dtype=jnp.bfloat16)
        to_slot = jax.nn.one_hot(slot, slots, dtype=jnp.bfloat16)
        weighted = to_expert * gate[..., None].astype(jnp.bfloat16)
        dispatch = einsum("abtke,abtkc->abtec", to_expert, to_slot).astype(jnp.bfloat16)
        combine = einsum("abtke,abtkc->abtec", weighted, to_slot).astype(jnp.bfloat16)
        z = einsum("abtec,abtd->aebcd", dispatch, x).astype(jnp.bfloat16)
        z = placed(z, "dp", None, "ep", None, None)
        z = placed(z, "dp", "ep", None, None, None)
        h = jax.nn.silu(einsum("aebcd,edf->aebcf", z, w_gate))
        h = (h * einsum("aebcd,edf->aebcf", z, w_up)).astype(jnp.bfloat16)
        out = einsum("aebcf,efd->aebcd", h, w_down).astype(jnp.bfloat16)
        out = placed(out, "dp", "ep", None, None, None)
        out = placed(out, "dp", None, "ep", None, None)
        y = einsum("abtec,aebcd->abtd", combine, out)
        return y.astype(jnp.bfloat16)

    return step
```

profile of v0, /device:TPU:112, one launch (start us, length us, event | category | flops | bytes accessed | tf_op | source)
XLA Modules:
  0.0 529.5 jit_solution(8471804139273259104)
XLA Ops:
  0.0 0.0 copy-start
  0.0 0.9 copy.3
  0.9 0.0 copy-start.2
  1.0 0.8 copy.5
  1.8 0.0 copy-done.2
  1.8 0.0 copy-start.4
  1.8 0.6 copy-done.4
  2.5 2.0 fusion.34
  4.5 0.8 copy.9
  5.3 0.0 copy-done
  5.3 2.2 convert_bitcast_fusion.1
  7.5 98.3 %all-to-all.4 = bf16[1,16,1,1,80,3072]{5,4,3,2,0,1:T(8,128)(2,1)S(1)} all-to-all(bf16[1,16,1,1,80,3072]{5,4,3,2,0,1:T(8,128)(2,1)S(1)} %convert_bitcast_fusion.1), channel_id=1, replica_groups=mesh['dp'=2,'ep'=16] {'ep'}, dimensions={1} | all-to-all | bytes 15728640 | tf_op jit(solution)/sharding_constraint;jit(solution)/sharding_constraint | solution.py:13
  105.8 94.4 %fusion.2 = f32[16,80,10752]{2,1,0:T(8,128)} fusion(bf16[1,3072,10752]{2,1,0:T(8,128)(2,1)} %param.5, bf16[1,16,1,1,80,3072]{5,4,3,2,0,1:T(8,128)(2,1)S(1)} %all-to-all.4), kind=kOutput, calls=%fused_computation.2 | convolution fusion | flops 84557168640 | bytes 128974848 | tf_op jit(solution)/aebcd,edf->aebcf/dot_general | solution.py:8
  200.2 94.5 %fusion.4 = f32[16,80,10752]{2,1,0:T(8,128)} fusion(bf16[1,3072,10752]{2,1,0:T(8,128)(2,1)} %param.4, bf16[1,16,1,1,80,3072]{5,4,3,2,0,1:T(8,128)(2,1)S(1)} %all-to-all.4), kind=kOutput, calls=%fused_computation.4 | convolution fusion | flops 84557168640 | bytes 128974848 | tf_op jit(solution)/aebcd,edf->aebcf/dot_general | solution.py:8
  294.7 0.0 copy-start.6
  294.7 0.0 copy-start.3
  294.7 0.0 copy-start.5
  294.7 0.0 copy-start.1
  294.7 99.8 %convert_bitcast_fusion = bf16[1,1,16,1,80,3072]{5,4,3,1,0,2:T(8,128)(2,1)} fusion(bf16[1,10752,3072]{2,1,0:T(8,128)(2,1)} %param.6, f32[16,80,10752]{2,1,0:T(8,128)} %fusion.2, f32[16,80,10752]{2,1,0:T(8,128)} %fusion.4), kind=kOutput, calls=%fused_computation.18 | convolution fusion | flops 84643676160 | bytes 184025088 | tf_op jit(solution)/aebcf,efd->aebcd/dot_general | solution.py:8
  394.6 9.0 %all-to-all-start.1 = ((bf16[1,1,16,1,80,3072]{5,4,3,1,0,2:T(8,128)(2,1)}), bf16[1,1,16,1,80,3072]{5,4,3,1,0,2:T(8,128)(2,1)}, u32[]{:S(2)}, u32[]{:S(2)}) async-start(bf16[1,1,16,1,80,3072]{5,4,3,1,0,2:T(8,128)(2,1)} %convert_bitcast_fusion), calls=%async_computation.1 | async-start | bytes 15728640 | tf_op jit(solution)/sharding_constraint;jit(solution)/sharding_constraint | solution.py:13
  403.6 0.0 copy-done.6
  403.6 0.1 copy.4
  403.7 0.0 copy-done.3
  403.7 0.0 copy-done.5
  403.7 2.4 fusion.38
  406.2 0.8 copy.8
  407.0 115.9 %all-to-all-done.1 = bf16[1,1,16,1,80,3072]{5,4,3,1,0,2:T(8,128)(2,1)} async-done(((bf16[1,1,16,1,80,3072]{5,4,3,1,0,2:T(8,128)(2,1)}), bf16[1,1,16,1,80,3072]{5,4,3,1,0,2:T(8,128)(2,1)}, u32[]{:S(2)}, u32[]{:S(2)}) %all-to-all-start.1) | async-done | bytes 7864352 | tf_op jit(solution)/sharding_constraint;jit(solution)/sharding_constraint | solution.py:13
  522.9 6.6 %fusion.26 = bf16[1,1,256,3072]{3,2,1,0:T(8,128)(2,1)} fusion(bf16[1,1,16,1,80,3072]{5,4,3,1,0,2:T(8,128)(2,1)} %all-to-all-done.1, bf16[256,16,80]{0,2,1:T(8,128)(2,1)S(1)} %copy.8), kind=kOutput, calls=%fused_computation.22 | convolution fusion | flops 2014052352 | bytes 10092544 | tf_op jit(solution)/abtec,aebcd->abtd/dot_general | solution.py:8
  529.5 0.0 copy-done.1
  (1 shorter events, 0.0 us)
Async XLA Ops:
  0.0 5.3 copy-start
  0.9 0.9 copy-start.2
  1.8 0.7 copy-start.4
  294.7 108.9 %copy-start.6 = (f32[1,1,256,4]{2,3,1,0:T(4,128)S(1)}, f32[1,1,256,4]{2,3,1,0:T(4,128)}, u32[]{:S(2)}) copy-start(f32[1,1,256,4]{2,3,1,0:T(4,128)} %param.1) | copy-start | bytes 12292
  294.7 109.0 %copy-start.3 = (s32[256,4]{1,0:T(8,128)S(1)}, s32[256,4]{1,0:T(8,128)}, u32[]{:S(2)}) copy-start(s32[256,4]{1,0:T(8,128)} %copy-done.2) | copy-start | bytes 12292
  294.7 109.0 %copy-start.5 = (s32[256,4]{1,0:T(8,128)S(1)}, s32[256,4]{1,0:T(8,128)}, u32[]{:S(2)}) copy-start(s32[256,4]{1,0:T(8,128)} %copy-done.4) | copy-start | bytes 12292
  294.7 234.8 %copy-start.1 = (bf16[1,1,256,3072]{3,2,1,0:T(8,128)(2,1)S(1)}, bf16[1,1,256,3072]{3,2,1,0:T(8,128)(2,1)}, u32[]{:S(2)}) copy-start(bf16[1,1,256,3072]{3,2,1,0:T(8,128)(2,1)} %param.3) | copy-start | bytes 4718596
  394.6 128.4 %all-to-all-start.1 = ((bf16[1,1,16,1,80,3072]{5,4,3,1,0,2:T(8,128)(2,1)}), bf16[1,1,16,1,80,3072]{5,4,3,1,0,2:T(8,128)(2,1)}, u32[]{:S(2)}, u32[]{:S(2)}) async-start(bf16[1,1,16,1,80,3072]{5,4,3,1,0,2:T(8,128)(2,1)} %convert_bitcast_fusion), calls=%async_computation.1 | async-start | bytes 15728640 | tf_op jit(solution)/sharding_constraint;jit(solution)/sharding_constraint | solution.py:13
where the time goes:
time: 530 us
  matrix products  302 us (57%)
  waiting for transfers between devices  116 us (22%)
  blocking collectives  98.3 us (19%)
  starting transfers between devices  9.01 us (2%)
    dot_general x7, matrix products, einsum(): return jnp.einsum(form, a.astype(jnp.float32), b.astype(jnp.float32))  302 us
    another operation x1, waiting for transfers between devices, placed(): return lax.with_sharding_constraint(v, NamedSharding(mesh, P(*spec)))  116 us
    another operation x1, blocking collectives, placed(): return lax.with_sharding_constraint(v, NamedSharding(mesh, P(*spec)))  98.3 us
  transfers between devices with their start and end apart: 1, of which 1 were waited for; matrix products, arithmetic and copies ran while one was open for 1% of the time, Pallas kernels for 0%

commit v1 on v0

v1 whole, which is shorter than its diff:
```python
import functools
import math

import jax
import jax.numpy as jnp
from jax import lax
from jax.experimental import pallas as pl
from jax.experimental.pallas import tpu as pltpu
from jax.sharding import PartitionSpec as P

MESH = pl.DeviceIdType.MESH
F32, BF16 = jnp.float32, jnp.bfloat16
COLS = 256
PAIRS = 2
RING = 3


def plan(side):
    far = lambda v: min(v, side - v)
    peers = sorted(((far(a) + far(b), a, b) for a in range(side) for b in range(side)))
    near = [(a, b) for n, a, b in peers if n <= 1]
    mid = [(a, b) for n, a, b in peers if n == 2]
    rest = [(a, b) for n, a, b in peers if n > 2]
    return near, mid, rest


def kernel(
    side, slots, x_ref, expert_ref, slot_ref, gate_ref, wg_ref, wu_ref, wd_ref, y_ref,
    z, h, back, w, comb, x_sem, w_sem, y_sem, out_s, out_r, far_s, far_r, end_s, end_r,
):
    tokens, d = x_ref.shape
    ff = wd_ref.shape[0]
    near, mid, rest = plan(side)
    order = near + mid + rest
    where = {o: p for p, o in enumerate(order)}
    mirror = [where[(-a) % side, (-b) % side] for a, b in order]
    members = len(order)
    n_near, n_end = len(near), len(near) + len(mid)
    rows = lambda lo, hi: pl.ds(lo * slots, (hi - lo) * slots)
    me = lax.axis_index("ep")
    my_x, my_y = me // side, lax.rem(me, side)

    def device(p):
        a, b = order[p]
        return {"ep": lax.rem(my_x + a, side) * side + lax.rem(my_y + b, side)}

    barrier = pltpu.get_barrier_semaphore()
    for p in range(1, members):
        pl.semaphore_signal(barrier, inc=1, device_id=device(p), device_id_type=MESH)

    x_at = h.at[pl.ds(n_near * slots, tokens), pl.ds(d, d)]
    x_copy = pltpu.make_async_copy(x_ref, x_at, x_sem)
    x_copy.start()

    def staged(p):
        if p < n_near:
            return h.at[rows(n_near + p - 1, n_near + p), pl.ds(2 * d, d)]
        return h.at[rows(p, p + 1), pl.ds(0, d)]

    n_up, n_down = ff // (COLS * PAIRS), d // COLS
    steps = [n_up, n_up, n_down, n_up, n_down]

    def tile_up(i, s):
        for k in range(PAIRS):
            at = pl.ds(pl.multiple_of((i * PAIRS + k) * COLS, COLS), COLS)
            pltpu.make_async_copy(wg_ref.at[:, at], w.at[s, pl.ds(2 * k * d, d)], w_sem.at[s]).start()
            pltpu.make_async_copy(wu_ref.at[:, at], w.at[s, pl.ds((2 * k + 1) * d, d)], w_sem.at[s]).start()

    def tile_down(i, s):
        at = pl.ds(pl.multiple_of(i * COLS, COLS), COLS)
        pltpu.make_async_copy(wd_ref.at[:, at], w.at[s, pl.ds(0, ff)], w_sem.at[s]).start()

    fetch = [tile_up, tile_up, tile_down, tile_up, tile_down]
    taken = [2 * PAIRS * d, 2 * PAIRS * d, ff, 2 * PAIRS * d, ff]
    for i in range(RING - 1):
        tile_up(i, i)

    def phase(k, lo, hi, body):
        n, first = steps[k], sum(steps[:k])

        def step(i, carry):
            s = lax.rem(i + first, RING)
            got = w.at[s, pl.ds(0, taken[k])]
            pltpu.make_async_copy(got, got, w_sem.at[s]).wait()
            ahead = i + RING - 1
            s_ahead = lax.rem(ahead + first, RING)

            @pl.when(ahead < n)
            def _():
                fetch[k](ahead, s_ahead)

            if k + 1 < len(steps):

                @pl.when(ahead >= n)
                def _():
                    fetch[k + 1](ahead - n, s_ahead)

            body(i, s)
            return carry

        lax.fori_loop(lo, hi, step, 0)

    expert, slot = expert_ref[...], slot_ref[...]
    off = lax.rem(expert // side - my_x + side, side) * side + lax.rem(lax.rem(expert, side) - my_y + side, side)
    place = jnp.zeros_like(off)
    for p, (a, b) in enumerate(order):
        place = jnp.where(off == a * side + b, p, place)
    code = jnp.where(slot < slots, place * slots + slot, -1)
    gate = gate_ref[...].astype(BF16).astype(F32)

    def chosen(lo, n, value):
        row = lax.broadcasted_iota(jnp.int32, (n, tokens), 0) + lo
        out = jnp.zeros((n, tokens), F32)
        for j in range(code.shape[0]):
            out = jnp.where(row == code[j : j + 1, :], value(j), out)
        return out

    def block_rows(lo, hi, at):
        pick = chosen(lo * slots, (hi - lo) * slots, lambda j: 1.0).astype(BF16)
        for c in range(0, d, 2 * COLS):
            cols = pl.ds(c, min(2 * COLS, d - c))
            got = jnp.dot(pick, x_at[:, cols], preferred_element_type=F32).astype(BF16)
            for p in range(lo, hi):
                at(p)[:, cols] = got[(p - lo) * slots : (p - lo + 1) * slots]

    def send(p):
        return pltpu.make_async_remote_copy(
            src_ref=staged(p),
            dst_ref=z.at[rows(mirror[p], mirror[p] + 1)],
            send_sem=out_s.at[p],
            recv_sem=out_r.at[mirror[p]],
            device_id=device(p),
            device_id_type=MESH,
        )

    def arrived(lo, hi):
        for p in range(lo, hi):
            got = z.at[rows(p, p + 1)]
            pltpu.make_async_copy(got, got, out_r.at[p]).wait()

    x_copy.wait()
    block_rows(1, n_near, staged)
    pl.semaphore_wait(barrier, members - 1)
    for p in range(1, n_near):
        send(p).start()
    block_rows(n_end, members, staged)
    for p in range(n_end, members):
        send(p).start()
    block_rows(n_near, n_end, staged)
    for p in range(n_near, n_end):
        send(p).start()
    block_rows(0, 1, lambda p: z.at[rows(0, 1)])
    for c in range(0, members * slots, 128):
        part = chosen(c, 128, lambda j: gate[j : j + 1, :])
        comb[:, pl.ds(c, 128)] = part.T.astype(BF16)

    def up(lo, hi):
        at = rows(lo, hi)

        def body(i, s):
            for k in range(PAIRS):
                g = jnp.dot(z[at, :], w[s, pl.ds(2 * k * d, d)], preferred_element_type=F32)
                u = jnp.dot(z[at, :], w[s, pl.ds((2 * k + 1) * d, d)], preferred_element_type=F32)
                cols = pl.ds(pl.multiple_of((i * PAIRS + k) * COLS, COLS), COLS)
                h[at, cols] = (jax.nn.silu(g) * u).astype(BF16)

        return body

    def result(p, c, send_sem, recv_sem):
        cols = pl.ds(pl.multiple_of(c * COLS, COLS), COLS)
        return pltpu.make_async_remote_copy(
            src_ref=z.at[rows(p, p + 1), cols],
            dst_ref=back.at[rows(mirror[p], mirror[p] + 1), cols],
            send_sem=send_sem,
            recv_sem=recv_sem,
            device_id=device(p),
            device_id_type=MESH,
        )

    def down_rest(i, s):
        at = rows(n_end, members)
        cols = pl.ds(pl.multiple_of(i * COLS, COLS), COLS)
        out = jnp.dot(h[at, :], w[s, pl.ds(0, ff)], preferred_element_type=F32)
        z[at, cols] = out.astype(BF16)
        for p in range(n_end, members):
            result(p, i, far_s, far_r).start()

    def down_end(i, s):
        cols = pl.ds(pl.multiple_of(i * COLS, COLS), COLS)
        out = jnp.dot(h[rows(0, n_end), :], w[s, pl.ds(0, ff)], preferred_element_type=F32).astype(BF16)
        back[rows(0, 1), cols] = out[:slots]
        z[rows(1, n_end), cols] = out[slots:]
        for p in range(n_near, n_end):
            result(p, i, end_s, end_r.at[i]).start()
        for p in range(1, n_near):
            result(p, i, end_s, end_r.at[i]).start()

    arrived(1, n_near)
    phase(0, 0, n_up, up(0, n_near))
    arrived(n_end, members)
    for p in range(n_end, members):
        send(p).wait_send()
    phase(1, 0, n_up, up(n_end, members))
    phase(2, 0, n_down, down_rest)
    arrived(n_near, n_end)
    for p in range(1, n_end):
        send(p).wait_send()
    phase(3, 0, n_up, up(n_near, n_end))
    phase(4, 0, n_down, down_end)

    got = back.at[rows(n_end, members)]
    pltpu.make_async_copy(got, got, far_r).wait()
    writes = []
    for c in range(n_down):
        cols = pl.ds(c * COLS, COLS)
        got = back.at[rows(1, n_end), cols]
        pltpu.make_async_copy(got, got, end_r.at[c]).wait()
        total = jnp.dot(comb[...], back[:, cols], preferred_element_type=F32)
        kept = w.at[0, pl.ds(c * tokens, tokens)]
        kept[...] = total.astype(BF16)
        write = pltpu.make_async_copy(kept, y_ref.at[:, cols], y_sem)
        write.start()
        writes.append(write)
    for write in writes:
        write.wait()
    gone = z.at[rows(n_end, members)]
    pltpu.make_async_copy(gone, gone, far_s).wait()
    gone = z.at[rows(1, n_end)]
    pltpu.make_async_copy(gone, gone, end_s).wait()


def solution(mesh):
    members = mesh.shape["ep"]
    side = math.isqrt(members)

    def layer(x, expert, slot, gate, w_gate, w_up, w_down):
        tokens, d = x.shape[2:]
        ff, top = w_gate.shape[2], expert.shape[3]
        slots = 5 * tokens * top // (4 * members)
        total = members * slots
        any_ = pl.BlockSpec(memory_space=pl.ANY)
        vmem = pl.BlockSpec(memory_space=pltpu.VMEM)
        turned = lambda v: v.reshape(tokens, top).T
        y = pl.pallas_call(
            functools.partial(kernel, side, slots),
            out_shape=jax.ShapeDtypeStruct((tokens, d), BF16),
            in_specs=[any_, vmem, vmem, vmem, any_, any_, any_],
            out_specs=any_,
            scratch_shapes=[
                pltpu.VMEM((total, d), BF16),
                pltpu.VMEM((total, ff), BF16),
                pltpu.VMEM((total, d), BF16),
                pltpu.VMEM((RING, max(2 * PAIRS * d, ff), COLS), BF16),
                pltpu.VMEM((tokens, total), BF16),
                pltpu.SemaphoreType.DMA,
                pltpu.SemaphoreType.DMA((RING,)),
                pltpu.SemaphoreType.DMA,
                pltpu.SemaphoreType.DMA((members,)),
                pltpu.SemaphoreType.DMA((members,)),
                pltpu.SemaphoreType.DMA,
                pltpu.SemaphoreType.DMA,
                pltpu.SemaphoreType.DMA,
                pltpu.SemaphoreType.DMA((d // COLS,)),
            ],
            compiler_params=pltpu.CompilerParams(
                collective_id=0, has_side_effects=True, vmem_limit_bytes=67_043_328
            ),
            name="moe",
        )(
            x.reshape(tokens, d), turned(expert), turned(slot), turned(gate),
            w_gate.reshape(d, ff), w_up.reshape(d, ff), w_down.reshape(ff, d),
        )
        return y.reshape(1, 1, tokens, d)

    per_device, per_expert = P("dp", "ep", None, None), P("ep", None, None)
    return jax.shard_map(
        layer,
        mesh=mesh,
        in_specs=(per_device,) * 4 + (per_expert,) * 3,
        out_specs=per_device,
        check_vma=False,
    )
```

time: 530 us -> 349 us (0.66)
  the two profiles are of different devices: /device:TPU:112 before, /device:TPU:97 now
where the time goes in v1:
time: 349 us; the launch traced here: 348 us
  Pallas kernels  345 us (99%)
    pallas_call x1, Pallas kernels, layer(): pl.pallas_call(functools.partial(kernel, side, slots), out_shape=jax.Shap...  345 us

profile of v1, /device:TPU:97, one launch (start us, length us, event | category | flops | bytes accessed | tf_op | source)
XLA Modules:
  0.0 347.7 jit_solution(6092721544115327203)
XLA Ops:
  0.0 345.0 %moe.1 = bf16[256,3072]{1,0:T(8,128)(2,1)} custom-call(bf16[256,3072]{1,0:T(8,128)(2,1)} %bitcast.18, s32[4,256]{1,0:T(4,128)} %bitcast.19, s32[4,256]{1,0:T(4,128)} %bitcast.20, f32[4,256]{1,0:T(4,128)} %bitcast.21, bf16[3072,10752]{1,0:T(8,128)(2,1)} %bitcast.14, bf16[3072,10752]{1,0:T(8,128)(2,1)} %bitcast.15, bf16[10752,3072]{1,0:T(8,128)(2,1)} %bitcast.16), custom_call_target="tpu_custom_call" | custom-call | tf_op jit(solution)/shard_map/moe/pallas_call | solution.py:244
  345.0 2.7 copy.9
